TPU v7x, 128 devices: a whole 4x4x4 slice. The times are simulated.
128 devices in a mesh: expert: 4 (over y_lo, core), shard: 32 (over z, y_hi, x).
Axes of the slice: x: 4, y: 4 (y_hi: 2, y_lo: 2; y = y_hi * 2 + y_lo), z: 4, core: 2. Of those that a mesh axis runs over, the one named last changes fastest.
Arguments:
- master_gate: float32 [128, 2048, 768], P('expert', 'shard'), may hold values from -0.125 to 0.125
- second_gate: bfloat16 [128, 2048, 768], P('expert', 'shard'), may hold values from -0.0625 to 0.0625
- master_up: float32 [128, 2048, 768], P('expert', 'shard'), may hold values from -0.125 to 0.125
- second_up: bfloat16 [128, 2048, 768], P('expert', 'shard'), may hold values from -0.0625 to 0.0625
- router_weight: float32 [2048, 128], P('shard', 'expert'), may hold values from -0.125 to 0.125
- router_gain: float32 [2048], P('shard'), may hold values from 0.25 to 1.75
Outputs:
- final_gate: bfloat16 [128, 768, 2048], P('expert', 'shard')
- final_up: bfloat16 [128, 768, 2048], P('expert', 'shard')
- serve_router: bfloat16 [2048, 128], replicated
All inputs are finite; a program needn't handle non-finite values.
Results may differ from a plain program's by a relative error of at most 0.001.
Values may be sent and summed in bfloat16 or wider, within the bound.
No kernel may reach another device: no remote copies, remote signals or barrier semaphores. Data moves between devices by JAX's collectives and lax.ppermute only.
A program may use at most 128 MiB of HBM per device.

v0:
```python
import jax
import jax.numpy as jnp
from jax import lax
from jax.sharding import PartitionSpec as P


def from_everyone(x, axis):
    devices = lax.axis_size(axis)
    return lax.all_to_all(jnp.broadcast_to(x[None], (devices, *x.shape)), axis, 0, 0, tiled=True)


def in_order(pieces, dim):
    pieces = jnp.moveaxis(pieces, 0, dim)
    lengths = pieces.shape
    return pieces.reshape(*lengths[:dim], lengths[dim] * lengths[dim + 1], *lengths[dim + 2 :])


def gathered_copies(x, axis, dim):
    pieces = from_everyone(x, axis)
    return in_order(pieces, dim)


def per_device(master_gate, second_gate, master_up, second_up, router_weight, router_gain):
    merged_gate = master_gate + second_gate.astype(jnp.float32)
    merged_up = master_up + second_up.astype(jnp.float32)
    narrow_gate, narrow_up = (merged_gate.astype(jnp.bfloat16), merged_up.astype(jnp.bfloat16))
    final_gate, final_up = (
        lax.all_to_all(narrow_gate, "shard", split_axis=2, concat_axis=1, tiled=True),
        lax.all_to_all(narrow_up, "shard", split_axis=2, concat_axis=1, tiled=True),
    )
    final_gate = jnp.transpose(final_gate, (0, 2, 1))
    final_up = jnp.transpose(final_up, (0, 2, 1))
    part_router = (router_weight * router_gain[:, None]).astype(jnp.bfloat16)
    row_router = gathered_copies(part_router, "shard", 0)
    serve_router = gathered_copies(row_router, "expert", 1)
    return (final_gate, final_up, serve_router)


def solution(mesh):
    placed = (
        P("expert", "shard", None),
        P("expert", "shard", None),
        P("expert", "shard", None),
        P("expert", "shard", None),
        P("shard", "expert"),
        P("shard"),
    )
    return jax.shard_map(
        per_device,
        mesh=mesh,
        in_specs=placed,
        out_specs=(P("expert", "shard", None), P("expert", "shard", None), P()),
        check_vma=False,
    )
```

profile of v0, /device:TPU:18, one launch (start us, length us, event | category | flops | bytes accessed | tf_op | source)
XLA Modules:
  0.0 180.8 jit_solution(13884537367566639858)
XLA Ops:
  0.6 0.7 multiply_convert_fusion
  1.4 0.2 reshape.17
  1.6 17.4 %all_to_all.46 = bf16[32,2,1024]{2,1,0:T(2,128)(2,1)S(1)} all-to-all(bf16[32,2,1024]{2,1,0:T(2,128)(2,1)S(1)} %reshape.17), channel_id=1, replica_groups=mesh['expert'=4,'shard'=32] {'shard'}, dimensions={0} | all-to-all | bytes 262144 | tf_op jit(solution)/shard_map/all_to_all | solution.py:9
  18.9 0.2 reshape.18
  19.2 0.1 copy.49
  19.3 0.3 broadcast_in_dim.7
  19.6 0.9 broadcast_in_dim.16
  20.4 4.1 %all-to-all-start.3 = ((bf16[4,2048,32]{1,2,0:T(8,128)(2,1)}), bf16[4,2048,32]{1,2,0:T(8,128)(2,1)}, u32[]{:S(2)}, u32[]{:S(2)}) async-start(bf16[4,2048,32]{1,2,0:T(8,128)(2,1)} %broadcast_in_dim.16), calls=%async_computation.3 | async-start | bytes 1048576 | tf_op jit(solution)/shard_map/all_to_all | solution.py:9
  24.6 4.7 %add_convert_fusion.1 = bf16[32,64,768]{2,1,0:T(8,128)(2,1)S(1)} fusion(f32[32,64,768]{2,1,0:T(8,128)} %param.6, bf16[32,64,768]{2,1,0:T(8,128)(2,1)} %param.7), kind=kLoop, calls=%fused_computation.1 | loop fusion | flops 4718592 | bytes 12582912 | tf_op jit(solution)/shard_map/convert_element_type | solution.py:26
  29.3 9.5 %copy.43 = bf16[32,64,768]{1,0,2:T(8,128)(2,1)} copy(bf16[32,64,768]{2,1,0:T(8,128)(2,1)S(1)} %add_convert_fusion.1) | data formatting | bytes 6291456 | tf_op jit(solution)/shard_map/convert_element_type | solution.py:26
  38.8 8.7 %reshape.13 = bf16[32,2,24576]{2,1,0:T(2,128)(2,1)} reshape(bf16[768,32,64]{2,1,0:T(8,128)(2,1)} %bitcast.28) | data formatting | bytes 6291456
  47.5 0.0 all-to-all-done.3
  47.5 7.5 %all-to-all-start = ((bf16[32,2,24576]{2,1,0:T(2,128)(2,1)}), bf16[32,2,24576]{2,1,0:T(2,128)(2,1)S(1)}, u32[]{:S(2)}, u32[]{:S(2)}) async-start(bf16[32,2,24576]{2,1,0:T(2,128)(2,1)} %reshape.13), calls=%async_computation | async-start | bytes 6291456 | tf_op jit(solution)/shard_map/all_to_all | solution.py:28
  55.1 6.4 %add_convert_fusion = bf16[32,64,768]{2,1,0:T(8,128)(2,1)} fusion(f32[32,64,768]{2,1,0:T(8,128)} %param.8, bf16[32,64,768]{2,1,0:T(8,128)(2,1)} %param.9), kind=kLoop, calls=%fused_computation | loop fusion | flops 4718592 | bytes 12582912 | tf_op jit(solution)/shard_map/convert_element_type | solution.py:26
  61.5 10.2 %copy.46 = bf16[32,64,768]{1,0,2:T(8,128)(2,1)} copy(bf16[32,64,768]{2,1,0:T(8,128)(2,1)} %add_convert_fusion) | data formatting | bytes 6291456 | tf_op jit(solution)/shard_map/convert_element_type | solution.py:26
  71.7 8.7 %reshape.15 = bf16[32,2,24576]{2,1,0:T(2,128)(2,1)} reshape(bf16[768,32,64]{2,1,0:T(8,128)(2,1)} %bitcast.29) | data formatting | bytes 6291456
  80.4 21.7 %all-to-all-done = bf16[32,2,24576]{2,1,0:T(2,128)(2,1)S(1)} async-done(((bf16[32,2,24576]{2,1,0:T(2,128)(2,1)}), bf16[32,2,24576]{2,1,0:T(2,128)(2,1)S(1)}, u32[]{:S(2)}, u32[]{:S(2)}) %all-to-all-start) | async-done | bytes 3145760 | tf_op jit(solution)/shard_map/all_to_all | solution.py:28
  102.1 5.9 %all-to-all-start.1 = ((bf16[32,2,24576]{2,1,0:T(2,128)(2,1)}), bf16[32,2,24576]{2,1,0:T(2,128)(2,1)}, u32[]{:S(2)}, u32[]{:S(2)}) async-start(bf16[32,2,24576]{2,1,0:T(2,128)(2,1)} %reshape.15), calls=%async_computation.1 | async-start | bytes 6291456 | tf_op jit(solution)/shard_map/all_to_all | solution.py:29
  108.0 2.0 %copy.50 = bf16[2048,128]{1,0:T(8,128)(2,1)} copy(bf16[2048,128]{0,1:T(8,128)(2,1)} %bitcast.9) | data formatting | bytes 1048576
  110.1 6.2 %reshape.14 = bf16[768,32,64]{2,1,0:T(8,128)(2,1)} reshape(bf16[32,2,24576]{2,1,0:T(2,128)(2,1)S(1)} %all-to-all-done) | data formatting | bytes 6291456
  116.2 9.5 %copy.45 = bf16[32,32,64,24]{2,1,3,0:T(8,128)(2,1)} copy(bf16[32,32,64,24]{2,0,3,1:T(8,128)(2,1)} %bitcast.30) | data formatting | bytes 6291456 | tf_op jit(solution)/shard_map/all_to_all | solution.py:28
  125.7 9.7 %all_to_all.35 = bf16[32,2048,24]{1,2,0:T(8,128)(2,1)} reshape(bf16[32,32,64,24]{2,1,3,0:T(8,128)(2,1)} %copy.45) | data formatting | bytes 6291456 | tf_op jit(solution)/shard_map/all_to_all | solution.py:28
  135.4 17.5 %all-to-all-done.1 = bf16[32,2,24576]{2,1,0:T(2,128)(2,1)} async-done(((bf16[32,2,24576]{2,1,0:T(2,128)(2,1)}), bf16[32,2,24576]{2,1,0:T(2,128)(2,1)}, u32[]{:S(2)}, u32[]{:S(2)}) %all-to-all-start.1) | async-done | bytes 3145760 | tf_op jit(solution)/shard_map/all_to_all | solution.py:29
  152.9 8.7 %reshape.16 = bf16[768,32,64]{2,1,0:T(8,128)(2,1)} reshape(bf16[32,2,24576]{2,1,0:T(2,128)(2,1)} %all-to-all-done.1) | data formatting | bytes 6291456
  161.6 9.5 %copy.48 = bf16[32,32,64,24]{2,1,3,0:T(8,128)(2,1)} copy(bf16[32,32,64,24]{2,0,3,1:T(8,128)(2,1)} %bitcast.31) | data formatting | bytes 6291456 | tf_op jit(solution)/shard_map/all_to_all | solution.py:29
  171.1 9.7 %all_to_all.39 = bf16[32,2048,24]{1,2,0:T(8,128)(2,1)} reshape(bf16[32,32,64,24]{2,1,3,0:T(8,128)(2,1)} %copy.48) | data formatting | bytes 6291456 | tf_op jit(solution)/shard_map/all_to_all | solution.py:29
  (1 shorter events, 0.0 us)
Async XLA Ops:
  20.4 27.1 %all-to-all-start.3 = ((bf16[4,2048,32]{1,2,0:T(8,128)(2,1)}), bf16[4,2048,32]{1,2,0:T(8,128)(2,1)}, u32[]{:S(2)}, u32[]{:S(2)}) async-start(bf16[4,2048,32]{1,2,0:T(8,128)(2,1)} %broadcast_in_dim.16), calls=%async_computation.3 | async-start | bytes 1048576 | tf_op jit(solution)/shard_map/all_to_all | solution.py:9
  47.5 54.6 %all-to-all-start = ((bf16[32,2,24576]{2,1,0:T(2,128)(2,1)}), bf16[32,2,24576]{2,1,0:T(2,128)(2,1)S(1)}, u32[]{:S(2)}, u32[]{:S(2)}) async-start(bf16[32,2,24576]{2,1,0:T(2,128)(2,1)} %reshape.13), calls=%async_computation | async-start | bytes 6291456 | tf_op jit(solution)/shard_map/all_to_all | solution.py:28
  102.1 50.8 %all-to-all-start.1 = ((bf16[32,2,24576]{2,1,0:T(2,128)(2,1)}), bf16[32,2,24576]{2,1,0:T(2,128)(2,1)}, u32[]{:S(2)}, u32[]{:S(2)}) async-start(bf16[32,2,24576]{2,1,0:T(2,128)(2,1)} %reshape.15), calls=%async_computation.1 | async-start | bytes 6291456 | tf_op jit(solution)/shard_map/all_to_all | solution.py:29
where the time goes:
time: 182 us; the launch traced here: 181 us
  local copies, waits for them, and re-layouts  94.2 us (52%)
  waiting for transfers between devices  39.2 us (22%)
  starting transfers between devices  17.6 us (10%)
  blocking collectives  17.4 us (10%)
  other arithmetic  11.9 us (7%)
    unnamed x8, local copies, waits for them, and re-layouts  34.9 us
    all_to_all x1, waiting for transfers between devices, per_device(): lax.all_to_all(narrow_gate, 'shard', split_axis=2, concat_axis=1, tiled=T...  21.7 us
    all_to_all x2, local copies, waits for them, and re-layouts, per_device(): lax.all_to_all(narrow_up, 'shard', split_axis=2, concat_axis=1, tiled=True)  19.2 us
    all_to_all x2, local copies, waits for them, and re-layouts, per_device(): lax.all_to_all(narrow_gate, 'shard', split_axis=2, concat_axis=1, tiled=T...  19.2 us
    all_to_all x1, waiting for transfers between devices, per_device(): lax.all_to_all(narrow_up, 'shard', split_axis=2, concat_axis=1, tiled=True)  17.5 us
    all_to_all x1, blocking collectives, from_everyone(): lax.all_to_all(jnp.broadcast_to(x[None], (devices, *x.shape)), axis, 0, 0...  17.4 us
    convert_element_type x1, local copies, waits for them, and re-layouts, per_device(): merged_up.astype(jnp.bfloat16)  10.2 us
    convert_element_type x1, local copies, waits for them, and re-layouts, per_device(): merged_gate.astype(jnp.bfloat16)  9.47 us
  transfers between devices with their start and end apart: 3, of which 2 were waited for; matrix products, arithmetic and copies ran while one was open for 36% of the time, Pallas kernels for 0%

commit v1 on v0

v1 whole, which is shorter than its diff:
```python
import functools

import jax
import jax.numpy as jnp
from jax import lax
from jax.experimental import pallas as pl
from jax.experimental.pallas import tpu as pltpu
from jax.sharding import PartitionSpec as P

MIB = 1 << 20
IN_STEP = 2
OUT_STEP = 4


def joined(low, high):
    half = low.shape[-1] // 2
    return (
        jnp.concatenate([low[:, :half], high[:, :half]], axis=1),
        jnp.concatenate([low[:, half:], high[:, half:]], axis=1),
    )


def pack_kernel(part, master_gate, second_gate, master_up, second_up, weight, gain, send):
    experts, rows, width = master_gate.shape
    peers = width // part
    router = (weight[...] * gain[...]).astype(jnp.bfloat16)
    half = router.shape[0] // 2
    router = jnp.concatenate([router[:half], router[half:]], axis=1)
    for peer in range(peers):
        send[peer, experts * part :, :] = router

    def body(gate, gate_change, up, up_change):
        step = pl.program_id(0)
        for pair in range(IN_STEP // 2):
            for at, (master, second) in enumerate(((gate, gate_change), (up, up_change))):
                two = slice(2 * pair, 2 * pair + 2)
                merged = master[two] + second[two].astype(jnp.float32)
                turned = merged.reshape(2 * rows, width).T.astype(jnp.bfloat16)
                first = pl.multiple_of(step * (IN_STEP * part), 2 * part) + (2 * pair + at) * part
                for peer in range(peers):
                    send[peer, pl.ds(first, part), :] = turned[peer * part : (peer + 1) * part]

    block = pl.BlockSpec((IN_STEP, rows, width), lambda i: (i, 0, 0), pipeline_mode=pl.Buffered(4))
    pltpu.emit_pipeline(body, grid=(experts // IN_STEP,), in_specs=[block] * 4)(master_gate, second_gate, master_up, second_up)


def pack(master_gate, second_gate, master_up, second_up, weight, gain, peers):
    experts, rows, width = master_gate.shape
    part = width // peers
    lines = experts * part + weight.shape[0] // 2
    big = [pltpu.with_memory_space_constraint(x, pltpu.HBM) for x in (master_gate, second_gate, master_up, second_up)]
    in_hbm = pl.BlockSpec(memory_space=pltpu.HBM)
    in_vmem = pl.BlockSpec(memory_space=pltpu.VMEM)
    return pl.pallas_call(
        functools.partial(pack_kernel, part),
        in_specs=[in_hbm] * 4 + [in_vmem] * 2,
        out_specs=in_vmem,
        out_shape=pltpu.VMEM((peers, lines, 2 * rows), jnp.bfloat16),
        compiler_params=pltpu.CompilerParams(vmem_limit_bytes=32 * MIB),
        cost_estimate=pl.CostEstimate(flops=2 * master_gate.size, bytes_accessed=12 * master_gate.size, transcendentals=0),
        name="pack",
    )(*big, weight, gain)


def unpack_kernel(part, rows, taken, final_gate, final_up):
    peers = taken.shape[0]
    step = pl.program_id(0)
    for pair in range(OUT_STEP // 2):
        for at, final in enumerate((final_gate, final_up)):
            first = pl.multiple_of(step * (OUT_STEP * part), 2 * part) + (2 * pair + at) * part
            for couple in range(peers // 2):
                lanes = slice(2 * couple * rows, (2 * couple + 2) * rows)
                final[2 * pair, :, lanes], final[2 * pair + 1, :, lanes] = joined(
                    taken[2 * couple, pl.ds(first, part), :], taken[2 * couple + 1, pl.ds(first, part), :]
                )


def unpack(taken, experts, rows, part):
    peers = taken.shape[0]
    out = jax.ShapeDtypeStruct((experts, part, peers * rows), jnp.bfloat16)
    return pl.pallas_call(
        functools.partial(unpack_kernel, part, rows),
        grid=(experts // OUT_STEP,),
        in_specs=[pl.BlockSpec(memory_space=pltpu.VMEM)],
        out_specs=[pl.BlockSpec((OUT_STEP, part, peers * rows), lambda i: (i, 0, 0))] * 2,
        out_shape=[out, out],
        compiler_params=pltpu.CompilerParams(vmem_limit_bytes=32 * MIB),
        cost_estimate=pl.CostEstimate(flops=taken.size * 64, bytes_accessed=4 * taken.size, transcendentals=0),
        name="unpack",
    )(pltpu.with_memory_space_constraint(taken, pltpu.VMEM))


def router_kernel(*refs):
    *pieces, out, turned = refs
    me = lax.axis_index("expert")
    for other, piece in enumerate(pieces):
        peers, half, lanes = piece.shape
        first = pl.multiple_of((me ^ other) * (2 * half), 2 * half)
        for couple in range(peers // 2):
            columns = slice(couple * lanes, (couple + 1) * lanes)
            turned[pl.ds(first, half), columns], turned[pl.ds(first + half, half), columns] = joined(
                piece[2 * couple], piece[2 * couple + 1]
            )
    out[...] = turned[...].T


def spread_router(own):
    columns = lax.axis_size("expert")
    pieces = [own]
    for other in range(1, columns):
        pieces.append(lax.ppermute(own, "expert", [(i, i ^ other) for i in range(columns)]))
    peers, half, lanes = own.shape
    rows = peers * lanes // 2
    return pl.pallas_call(
        router_kernel,
        in_specs=[pl.BlockSpec(memory_space=pltpu.VMEM)] * columns,
        out_specs=pl.BlockSpec(memory_space=pltpu.VMEM),
        out_shape=jax.ShapeDtypeStruct((rows, columns * 2 * half), jnp.bfloat16),
        scratch_shapes=[pltpu.VMEM((columns * 2 * half, rows), jnp.bfloat16)],
        compiler_params=pltpu.CompilerParams(vmem_limit_bytes=16 * MIB),
        name="router",
    )(*pieces)


def per_device(master_gate, second_gate, master_up, second_up, router_weight, router_gain):
    experts, rows, width = master_gate.shape
    peers = lax.axis_size("shard")
    part = width // peers
    send = pack(master_gate, second_gate, master_up, second_up, router_weight.T, router_gain[None], peers)
    taken = lax.all_to_all(send, "shard", 0, 0, tiled=True)
    serve_router = spread_router(taken[:, experts * part :])
    final_gate, final_up = unpack(taken, experts, rows, part)
    return (final_gate, final_up, serve_router)


def solution(mesh):
    placed = (
        P("expert", "shard", None),
        P("expert", "shard", None),
        P("expert", "shard", None),
        P("expert", "shard", None),
        P("shard", "expert"),
        P("shard"),
    )
    return jax.shard_map(
        per_device,
        mesh=mesh,
        in_specs=placed,
        out_specs=(P("expert", "shard", None), P("expert", "shard", None), P()),
        check_vma=False,
    )
```

time: 182 us -> 107 us (0.59)
  the two profiles are of different devices: /device:TPU:18 before, /device:TPU:1 now
where the time goes in v1:
time: 107 us
  blocking collectives  86.8 us (81%)
  Pallas kernels  13.6 us (13%)
  starting transfers between devices  3.66 us (3%)
  local copies, waits for them, and re-layouts  1.37 us (1%)
    all_to_all x1, blocking collectives, per_device(): taken = lax.all_to_all(send, 'shard', 0, 0, tiled=True)  86.8 us
    pallas_call x1, Pallas kernels, pack(): pl.pallas_call(functools.partial(pack_kernel, part), in_specs=[in_hbm] *...  7.45 us
    pallas_call x1, Pallas kernels, unpack(): pl.pallas_call(functools.partial(unpack_kernel, part, rows), grid=(expert...  4.92 us
    ppermute x3, starting transfers between devices, spread_router(): lax.ppermute(own, 'expert', [(i, i ^ other) for i in range(columns)])  3.66 us
  transfers between devices with their start and end apart: 3, of which 1 were waited for; matrix products, arithmetic and copies ran while one was open for 0% of the time, Pallas kernels for 5%

profile of v1, /device:TPU:1, one launch (start us, length us, event | category | flops | bytes accessed | tf_op | source)
XLA Modules:
  0.0 106.9 jit_solution(2989402775473448570)
XLA Ops:
  0.6 0.0 copy-start
  0.6 0.7 copy-done
  1.4 0.0 copy-start.1
  1.4 0.7 copy-done.1
  2.0 7.5 %pack.1 = bf16[32,784,128]{2,1,0:T(8,128)(2,1)S(1)} custom-call(f32[32,64,768]{2,1,0:T(8,128)} %master_gate.1, bf16[32,64,768]{2,1,0:T(8,128)(2,1)} %second_gate.1, f32[32,64,768]{2,1,0:T(8,128)} %master_up.1, bf16[32,64,768]{2,1,0:T(8,128)(2,1)} %second_up.1, f32[32,64]{1,0:T(8,128)S(1)} %bitcast.2, f32[1,64]{1,0:T(1,128)S(1)} %bitcast.3), custom_call_target="tpu_custom_call" | custom-call | flops 3145728 | bytes 18874368 | tf_op jit(solution)/shard_map/pack/pallas_call | solution.py:54
  9.5 86.8 %all_to_all.5.taken = bf16[32,784,128]{2,1,0:T(8,128)(2,1)S(1)} all-to-all(bf16[32,784,128]{2,1,0:T(8,128)(2,1)S(1)} %pack.1), channel_id=1, replica_groups=mesh['expert'=4,'shard'=32] {'shard'}, dimensions={0} | all-to-all | bytes 12845056 | tf_op jit(solution)/shard_map/all_to_all | solution.py:130
  96.3 2.6 %collective-permute-start.2 = (bf16[32,16,128]{2,1,0:T(8,128)(2,1)S(1)}, bf16[32,16,128]{2,1,0:T(8,128)(2,1)S(1)}, u32[]{:S(2)}, u32[]{:S(2)}) collective-permute-start(bf16[32,16,128]{2,1,0:T(8,128)(2,1)S(1)} %slice.4.refs_0_), channel_id=1, source_target_pairs={{0,96},{32,64},{64,32},{96,0},{1,97},{33,65},{65,33},{97,1},{2,98}... | collective-permute-start | bytes 393224 | tf_op jit(solution)/shard_map/ppermute | solution.py:111
  98.9 1.1 collective-permute-start.1
  99.9 0.0 collective-permute-start
  99.9 4.9 %unpack.1 = (bf16[32,24,2048]{2,1,0:T(8,128)(2,1)}, bf16[32,24,2048]{2,1,0:T(8,128)(2,1)}) custom-call(bf16[32,784,128]{2,1,0:T(8,128)(2,1)S(1)} %all_to_all.5.taken), custom_call_target="tpu_custom_call" | custom-call | flops 205520896 | bytes 12845056 | tf_op jit(solution)/shard_map/unpack/pallas_call | solution.py:81
  104.9 0.0 collective-permute-done.2.refs_3_
  104.9 0.9 collective-permute-done.1.refs_2_
  105.7 0.0 collective-permute-done.refs_1_
  105.7 1.2 %router.1 = bf16[2048,128]{1,0:T(8,128)(2,1)} custom-call(bf16[32,16,128]{2,1,0:T(8,128)(2,1)S(1)} %slice.4.refs_0_, bf16[32,16,128]{2,1,0:T(8,128)(2,1)S(1)} %collective-permute-done.refs_1_, bf16[32,16,128]{2,1,0:T(8,128)(2,1)S(1)} %collective-permute-done.1.refs_2_, bf16[32,16,128]{2,1,0:T(8,128)(2,1)S(1)} %collective-permute-done.2.refs_3_), custom_call_target="tpu_custom_call" | custom-call | tf_op jit(solution)/shard_map/router/pallas_call | solution.py:114
  (1 shorter events, 0.0 us)
Async XLA Ops:
  0.6 0.7 copy-start
  1.4 0.7 copy-start.1
  96.3 8.6 %collective-permute-start.2 = (bf16[32,16,128]{2,1,0:T(8,128)(2,1)S(1)}, bf16[32,16,128]{2,1,0:T(8,128)(2,1)S(1)}, u32[]{:S(2)}, u32[]{:S(2)}) collective-permute-start(bf16[32,16,128]{2,1,0:T(8,128)(2,1)S(1)} %slice.4.refs_0_), channel_id=1, source_target_pairs={{0,96},{32,64},{64,32},{96,0},{1,97},{33,65},{65,33},{97,1},{2,98}... | collective-permute-start | bytes 393224 | tf_op jit(solution)/shard_map/ppermute | solution.py:111
  98.9 6.9 %collective-permute-start.1 = (bf16[32,16,128]{2,1,0:T(8,128)(2,1)S(1)}, bf16[32,16,128]{2,1,0:T(8,128)(2,1)S(1)}, u32[]{:S(2)}, u32[]{:S(2)}) collective-permute-start(bf16[32,16,128]{2,1,0:T(8,128)(2,1)S(1)} %slice.4.refs_0_), channel_id=1, source_target_pairs={{0,64},{32,96},{64,0},{96,32},{1,65},{33,97},{65,1},{97,33},{2,66}... | collective-permute-start | bytes 393224 | tf_op jit(solution)/shard_map/ppermute | solution.py:111
  99.9 5.8 %collective-permute-start = (bf16[32,16,128]{2,1,0:T(8,128)(2,1)S(1)}, bf16[32,16,128]{2,1,0:T(8,128)(2,1)S(1)}, u32[]{:S(2)}, u32[]{:S(2)}) collective-permute-start(bf16[32,16,128]{2,1,0:T(8,128)(2,1)S(1)} %slice.4.refs_0_), channel_id=1, source_target_pairs={{0,32},{32,0},{64,96},{96,64},{1,33},{33,1},{65,97},{97,65},{2,34}... | collective-permute-start | bytes 393224 | tf_op jit(solution)/shard_map/ppermute | solution.py:111

commit v2 on v1

--- a/solution.py
+++ b/solution.py
@@ -9,7 +9,7 @@
 
 MIB = 1 << 20
 IN_STEP = 2
-OUT_STEP = 4
+OUT_STEP = 8
 
 
 def joined(low, high):
@@ -20,14 +20,15 @@
     )
 
 
-def pack_kernel(part, master_gate, second_gate, master_up, second_up, weight, gain, send):
+def pack_kernel(part, master_gate, second_gate, master_up, second_up, far_weight, far_gain, send, weight, gain, come):
     experts, rows, width = master_gate.shape
     peers = width // part
-    router = (weight[...] * gain[...]).astype(jnp.bfloat16)
-    half = router.shape[0] // 2
-    router = jnp.concatenate([router[:half], router[half:]], axis=1)
-    for peer in range(peers):
-        send[peer, experts * part :, :] = router
+    fetches = (
+        pltpu.make_async_copy(far_weight, weight, come.at[0]),
+        pltpu.make_async_copy(far_gain, gain, come.at[1]),
+    )
+    for fetch in fetches:
+        fetch.start()
 
     def body(gate, gate_change, up, up_change):
         step = pl.program_id(0)
@@ -40,50 +41,83 @@
                 for peer in range(peers):
                     send[peer, pl.ds(first, part), :] = turned[peer * part : (peer + 1) * part]
 
-    block = pl.BlockSpec((IN_STEP, rows, width), lambda i: (i, 0, 0), pipeline_mode=pl.Buffered(4))
+    block = pl.BlockSpec((IN_STEP, rows, width), lambda i: (i, 0, 0), pipeline_mode=pl.Buffered(8))
     pltpu.emit_pipeline(body, grid=(experts // IN_STEP,), in_specs=[block] * 4)(master_gate, second_gate, master_up, second_up)
+    for fetch in fetches:
+        fetch.wait()
+    router = (weight[...] * gain[...]).astype(jnp.bfloat16)
+    half = router.shape[0] // 2
+    router = jnp.concatenate([router[:half], router[half:]], axis=1)
+    for peer in range(peers):
+        send[peer, experts * part :, :] = router
 
 
 def pack(master_gate, second_gate, master_up, second_up, weight, gain, peers):
     experts, rows, width = master_gate.shape
     part = width // peers
     lines = experts * part + weight.shape[0] // 2
-    big = [pltpu.with_memory_space_constraint(x, pltpu.HBM) for x in (master_gate, second_gate, master_up, second_up)]
+    big = [pltpu.with_memory_space_constraint(x, pltpu.HBM) for x in (master_gate, second_gate, master_up, second_up, weight, gain)]
     in_hbm = pl.BlockSpec(memory_space=pltpu.HBM)
     in_vmem = pl.BlockSpec(memory_space=pltpu.VMEM)
     return pl.pallas_call(
         functools.partial(pack_kernel, part),
-        in_specs=[in_hbm] * 4 + [in_vmem] * 2,
+        in_specs=[in_hbm] * 6,
         out_specs=in_vmem,
         out_shape=pltpu.VMEM((peers, lines, 2 * rows), jnp.bfloat16),
+        scratch_shapes=[
+            pltpu.VMEM(weight.shape, jnp.float32),
+            pltpu.VMEM(gain.shape, jnp.float32),
+            pltpu.SemaphoreType.DMA((2,)),
+        ],
         compiler_params=pltpu.CompilerParams(vmem_limit_bytes=32 * MIB),
         cost_estimate=pl.CostEstimate(flops=2 * master_gate.size, bytes_accessed=12 * master_gate.size, transcendentals=0),
         name="pack",
-    )(*big, weight, gain)
+    )(*big)
 
 
-def unpack_kernel(part, rows, taken, final_gate, final_up):
-    peers = taken.shape[0]
-    step = pl.program_id(0)
-    for pair in range(OUT_STEP // 2):
-        for at, final in enumerate((final_gate, final_up)):
-            first = pl.multiple_of(step * (OUT_STEP * part), 2 * part) + (2 * pair + at) * part
-            for couple in range(peers // 2):
-                lanes = slice(2 * couple * rows, (2 * couple + 2) * rows)
-                final[2 * pair, :, lanes], final[2 * pair + 1, :, lanes] = joined(
-                    taken[2 * couple, pl.ds(first, part), :], taken[2 * couple + 1, pl.ds(first, part), :]
-                )
+def unpack_kernel(part, taken, final_gate, final_up, ready_gate, ready_up, sent):
+    peers, _, lanes = taken.shape
+    experts = final_gate.shape[0]
+    steps = experts // OUT_STEP
+
+    def out(step, at):
+        ready, final = ((ready_gate, final_gate), (ready_up, final_up))[at]
+        some = pl.ds(step * OUT_STEP, OUT_STEP)
+        return pltpu.make_async_copy(ready.at[some], final.at[some], sent.at[at, step])
+
+    @pl.loop(0, steps)
+    def _(step):
+        for at, ready in enumerate((ready_gate, ready_up)):
+            for pair in range(OUT_STEP // 2):
+                first = pl.multiple_of(step * (OUT_STEP * part), 2 * part) + (2 * pair + at) * part
+                expert = step * OUT_STEP + 2 * pair
+                for couple in range(peers // 2):
+                    columns = slice(couple * lanes, (couple + 1) * lanes)
+                    ready[expert, :, columns], ready[expert + 1, :, columns] = joined(
+                        taken[2 * couple, pl.ds(first, part), :], taken[2 * couple + 1, pl.ds(first, part), :]
+                    )
+            out(step, at).start()
+
+    @pl.loop(0, steps)
+    def _(step):
+        out(step, 0).wait()
+        out(step, 1).wait()
 
 
 def unpack(taken, experts, rows, part):
     peers = taken.shape[0]
-    out = jax.ShapeDtypeStruct((experts, part, peers * rows), jnp.bfloat16)
+    shape = (experts, part, peers * rows)
+    out = jax.ShapeDtypeStruct(shape, jnp.bfloat16)
     return pl.pallas_call(
-        functools.partial(unpack_kernel, part, rows),
-        grid=(experts // OUT_STEP,),
+        functools.partial(unpack_kernel, part),
         in_specs=[pl.BlockSpec(memory_space=pltpu.VMEM)],
-        out_specs=[pl.BlockSpec((OUT_STEP, part, peers * rows), lambda i: (i, 0, 0))] * 2,
+        out_specs=[pl.BlockSpec(memory_space=pltpu.HBM)] * 2,
         out_shape=[out, out],
+        scratch_shapes=[
+            pltpu.VMEM(shape, jnp.bfloat16),
+            pltpu.VMEM(shape, jnp.bfloat16),
+            pltpu.SemaphoreType.DMA((2, experts // OUT_STEP)),
+        ],
         compiler_params=pltpu.CompilerParams(vmem_limit_bytes=32 * MIB),
         cost_estimate=pl.CostEstimate(flops=taken.size * 64, bytes_accessed=4 * taken.size, transcendentals=0),
         name="unpack",

time: 107 us -> 105 us (0.981)
  Pallas kernels: 13.6 us -> 11.5 us
  waiting for transfers between devices: 0.88 us -> 2.35 us
  local copies, waits for them, and re-layouts: 1.37 us -> 0.01 us
    pallas_call x1, Pallas kernels: 4.92 us -> 3.43 us  [unpack(): pl.pallas_call(functools.partial(unpack_kernel, part), in_specs=[pl.Block...]
    ppermute x3, waiting for transfers between devices: 0.88 us -> 2.35 us  [spread_router(): lax.ppermute(own, 'expert', [(i, i ^ other) for i in range(columns)])]
    unnamed x4 -> x0, local copies, waits for them, and re-layouts: 1.37 us -> none
  transfers between devices with their start and end apart: 3 -> 3, of which waited for: 1 -> 1; matrix products, arithmetic and copies ran while one was open for 0% -> 0% of each run, Pallas kernels for 5% -> 3%
where the time goes in v2:
time: 105 us
  blocking collectives  86.8 us (83%)
  Pallas kernels  11.5 us (11%)
  starting transfers between devices  3.66 us (3%)
  waiting for transfers between devices  2.35 us (2%)
    all_to_all x1, blocking collectives, per_device(): taken = lax.all_to_all(send, 'shard', 0, 0, tiled=True)  86.8 us
    pallas_call x1, Pallas kernels, pack(): pl.pallas_call(functools.partial(pack_kernel, part), in_specs=[in_hbm] *...  6.89 us
    ppermute x3, starting transfers between devices, spread_router(): lax.ppermute(own, 'expert', [(i, i ^ other) for i in range(columns)])  3.66 us
    pallas_call x1, Pallas kernels, unpack(): pl.pallas_call(functools.partial(unpack_kernel, part), in_specs=[pl.Block...  3.43 us
    ppermute x3, waiting for transfers between devices, spread_router(): lax.ppermute(own, 'expert', [(i, i ^ other) for i in range(columns)])  2.35 us
  transfers between devices with their start and end apart: 3, of which 1 were waited for; matrix products, arithmetic and copies ran while one was open for 0% of the time, Pallas kernels for 3%

profile of v2, /device:TPU:1, one launch (start us, length us, event | category | flops | bytes accessed | tf_op | source)
XLA Modules:
  0.0 105.0 jit_solution(10256694036917226425)
XLA Ops:
  0.6 6.9 %pack.1 = bf16[32,784,128]{2,1,0:T(8,128)(2,1)S(1)} custom-call(f32[32,64,768]{2,1,0:T(8,128)} %master_gate.1, bf16[32,64,768]{2,1,0:T(8,128)(2,1)} %second_gate.1, f32[32,64,768]{2,1,0:T(8,128)} %master_up.1, bf16[32,64,768]{2,1,0:T(8,128)(2,1)} %second_up.1, f32[32,64]{1,0:T(8,128)} %bitcast.2, f32[1,64]{1,0:T(1,128)} %bitcast.3), custom_call_target="tpu_custom_call" | custom-call | flops 3145728 | bytes 18874368 | tf_op jit(solution)/shard_map/pack/pallas_call | solution.py:62
  7.5 86.8 %all_to_all.5.taken = bf16[32,784,128]{2,1,0:T(8,128)(2,1)S(1)} all-to-all(bf16[32,784,128]{2,1,0:T(8,128)(2,1)S(1)} %pack.1), channel_id=1, replica_groups=mesh['expert'=4,'shard'=32] {'shard'}, dimensions={0} | all-to-all | bytes 12845056 | tf_op jit(solution)/shard_map/all_to_all | solution.py:164
  94.3 2.6 %collective-permute-start.2 = (bf16[32,16,128]{2,1,0:T(8,128)(2,1)S(1)}, bf16[32,16,128]{2,1,0:T(8,128)(2,1)S(1)}, u32[]{:S(2)}, u32[]{:S(2)}) collective-permute-start(bf16[32,16,128]{2,1,0:T(8,128)(2,1)S(1)} %slice.4.refs_0_), channel_id=1, source_target_pairs={{0,96},{32,64},{64,32},{96,0},{1,97},{33,65},{65,33},{97,1},{2,98}... | collective-permute-start | bytes 393224 | tf_op jit(solution)/shard_map/ppermute | solution.py:145
  96.9 1.1 %collective-permute-start.1 = (bf16[32,16,128]{2,1,0:T(8,128)(2,1)S(1)}, bf16[32,16,128]{2,1,0:T(8,128)(2,1)S(1)}, u32[]{:S(2)}, u32[]{:S(2)}) collective-permute-start(bf16[32,16,128]{2,1,0:T(8,128)(2,1)S(1)} %slice.4.refs_0_), channel_id=1, source_target_pairs={{0,64},{32,96},{64,0},{96,32},{1,65},{33,97},{65,1},{97,33},{2,66}... | collective-permute-start | bytes 393224 | tf_op jit(solution)/shard_map/ppermute | solution.py:145
  98.0 0.0 collective-permute-start
  98.0 3.4 %unpack.1 = (bf16[32,24,2048]{2,1,0:T(8,128)(2,1)}, bf16[32,24,2048]{2,1,0:T(8,128)(2,1)}) custom-call(bf16[32,784,128]{2,1,0:T(8,128)(2,1)S(1)} %all_to_all.5.taken), custom_call_target="tpu_custom_call" | custom-call | flops 205520896 | bytes 12845056 | tf_op jit(solution)/shard_map/unpack/pallas_call | solution.py:111
  101.4 0.0 collective-permute-done.2.refs_3_
  101.5 2.3 %collective-permute-done.1.refs_2_ = bf16[32,16,128]{2,1,0:T(8,128)(2,1)S(1)} collective-permute-done((bf16[32,16,128]{2,1,0:T(8,128)(2,1)S(1)}, bf16[32,16,128]{2,1,0:T(8,128)(2,1)S(1)}, u32[]{:S(2)}, u32[]{:S(2)}) %collective-permute-start.1) | collective-permute-done | bytes 131104 | tf_op jit(solution)/shard_map/ppermute | solution.py:145
  103.8 0.0 collective-permute-done.refs_1_
  103.8 1.2 %router.1 = bf16[2048,128]{1,0:T(8,128)(2,1)} custom-call(bf16[32,16,128]{2,1,0:T(8,128)(2,1)S(1)} %slice.4.refs_0_, bf16[32,16,128]{2,1,0:T(8,128)(2,1)S(1)} %collective-permute-done.refs_1_, bf16[32,16,128]{2,1,0:T(8,128)(2,1)S(1)} %collective-permute-done.1.refs_2_, bf16[32,16,128]{2,1,0:T(8,128)(2,1)S(1)} %collective-permute-done.2.refs_3_), custom_call_target="tpu_custom_call" | custom-call | tf_op jit(solution)/shard_map/router/pallas_call | solution.py:148
  (1 shorter events, 0.0 us)
Async XLA Ops:
  94.3 7.1 %collective-permute-start.2 = (bf16[32,16,128]{2,1,0:T(8,128)(2,1)S(1)}, bf16[32,16,128]{2,1,0:T(8,128)(2,1)S(1)}, u32[]{:S(2)}, u32[]{:S(2)}) collective-permute-start(bf16[32,16,128]{2,1,0:T(8,128)(2,1)S(1)} %slice.4.refs_0_), channel_id=1, source_target_pairs={{0,96},{32,64},{64,32},{96,0},{1,97},{33,65},{65,33},{97,1},{2,98}... | collective-permute-start | bytes 393224 | tf_op jit(solution)/shard_map/ppermute | solution.py:145
  96.9 6.9 %collective-permute-start.1 = (bf16[32,16,128]{2,1,0:T(8,128)(2,1)S(1)}, bf16[32,16,128]{2,1,0:T(8,128)(2,1)S(1)}, u32[]{:S(2)}, u32[]{:S(2)}) collective-permute-start(bf16[32,16,128]{2,1,0:T(8,128)(2,1)S(1)} %slice.4.refs_0_), channel_id=1, source_target_pairs={{0,64},{32,96},{64,0},{96,32},{1,65},{33,97},{65,1},{97,33},{2,66}... | collective-permute-start | bytes 393224 | tf_op jit(solution)/shard_map/ppermute | solution.py:145
  98.0 5.8 %collective-permute-start = (bf16[32,16,128]{2,1,0:T(8,128)(2,1)S(1)}, bf16[32,16,128]{2,1,0:T(8,128)(2,1)S(1)}, u32[]{:S(2)}, u32[]{:S(2)}) collective-permute-start(bf16[32,16,128]{2,1,0:T(8,128)(2,1)S(1)} %slice.4.refs_0_), channel_id=1, source_target_pairs={{0,32},{32,0},{64,96},{96,64},{1,33},{33,1},{65,97},{97,65},{2,34}... | collective-permute-start | bytes 393224 | tf_op jit(solution)/shard_map/ppermute | solution.py:145
